TPU v7x, 128 devices: a whole 4x4x4 slice. The times are simulated.
128 devices in a mesh: section: 32 (over y, x, core), tp: 4 (over z).
Axes of the slice: x: 4, y: 4, z: 4, core: 2. Of those that a mesh axis runs over, the one named last changes fastest.
Arguments:
- tokens_in: bfloat16 [2, 224, 7168], P(None, None, 'tp'), may hold values from -6 to 6
- norm_gain: float32 [2, 7168], P(None, 'tp'), may hold values from 0.5 to 2
- router_weight: float32 [2, 7168], P(None, 'tp'), may hold values from -0.0625 to 0.0625
- gate_weight: bfloat16 [32, 7168, 1152], P('section', 'tp'), may hold values from -0.0625 to 0.0625
- up_weight: bfloat16 [32, 7168, 1152], P('section', 'tp'), may hold values from -0.0625 to 0.0625
- down_weight: bfloat16 [32, 1152, 7168], P('section', None, 'tp'), may hold values from -0.046875 to 0.046875
- routed_rows: int32 [2, 2, 112], replicated, may hold values from 0 to 223, as said below
- routed_count: int32 [2, 2], replicated, may hold values from 56 to 112, as said below
Outputs:
- tokens_out: bfloat16 [2, 224, 7168], P(None, 'section', 'tp')
Inputs may be any that keep to these rules, and one draw needn't show every extreme that they name: `routed_rows`: within each microbatch and layer, the 112 entries are distinct token positions. Only the leading routed_count entries of a list are live; some list is full in every draw.
All inputs are finite; a program needn't handle non-finite values.
Results may differ from a plain program's by a relative error of at most 0.0074.
Values may be sent and summed in bfloat16 or wider, within the bound.
A program may use at most 64 MiB of HBM per device.

v0:
```python
import jax
import jax.numpy as jnp
from jax import lax
from jax.sharding import PartitionSpec as P

D = 7168
LAYERS = 2


EPSILON = 1e-06


def swapped(value, axis, distance):
    mask = 2**distance
    pairs = [(source, source ^ mask) for source in range(lax.axis_size(axis))]
    return lax.ppermute(value, axis, pairs)


def from_everyone(value, axis):
    copies = jnp.broadcast_to(value, (lax.axis_size(axis), *value.shape))
    return lax.all_to_all(copies, axis, split_axis=0, concat_axis=0, tiled=True)


def taken_together(value, axis):
    everything = from_everyone(value, axis)
    return jnp.sum(everything, axis=0)


def in_one(arrays, axis):
    ends = [0]
    for a in arrays:
        ends.append(ends[-1] + a.size)
    so_far = taken_together(jnp.concatenate([a.ravel() for a in arrays]), axis)
    return tuple((so_far[b:e].reshape(a.shape) for a, b, e in zip(arrays, ends, ends[1:])))


def in_one_piece(arrays, axis, dim, along):
    widths = [a.shape[along] for a in arrays]
    both = jnp.concatenate(arrays, axis=along)
    result = lax.psum_scatter(both, axis, scatter_dimension=dim, tiled=True)
    return tuple(jnp.split(result, [sum(widths[:k]) for k in range(1, len(widths))], axis=along))


def laid_out(blocks, dim):
    shape = list(blocks.shape[1:])
    shape[dim] *= blocks.shape[0]
    return jnp.moveaxis(blocks, 0, dim).reshape(shape)


def gather_directly(value, axis, dim):
    return laid_out(from_everyone(value, axis), dim)


def shifted(value, axis, by):
    length = lax.axis_size(axis)
    pairs = [(i, i + by) for i in range(length) if 0 <= i + by < length]
    return lax.ppermute(value, axis, pairs)


def cut_along(value, dim, length):
    shape = value.shape
    blocks = value.reshape(*shape[:dim], length, shape[dim] // length, *shape[dim + 1 :])
    return jnp.moveaxis(blocks, dim, 0)


def sent_and_summed(value, axis, dim):
    blocks = cut_along(value, dim, lax.axis_size(axis))
    arrived = lax.all_to_all(blocks, axis, split_axis=0, concat_axis=0, tiled=True)
    return arrived.astype(jnp.float32).sum(axis=0)


def on_device(
    tokens_in,
    norm_gain,
    router_weight,
    gate_weight,
    up_weight,
    down_weight,
    routed_rows,
    routed_count,
):
    micro_count, token_count, quarter = tokens_in.shape
    capacity = routed_rows.shape[2]
    section_index = lax.axis_index("section")
    group_size = lax.axis_size("section") // LAYERS
    bit_count = group_size.bit_length() - 1
    layer_index = section_index // group_size
    total_steps = micro_count + LAYERS - 1
    gain_row = norm_gain[layer_index]
    router_row = router_weight[layer_index]
    gate_block = gate_weight[0]
    up_block = up_weight[0]
    down_block = down_weight[0]

    def sum_groups(partial_value):
        piece = partial_value
        for bit in reversed(range(bit_count)):
            half = piece.shape[1] // 2
            upper_side = section_index // 2**bit % 2 == 1
            lower, upper = (piece[:, :half], piece[:, half:])
            keep = jnp.where(upper_side, upper, lower)
            give = jnp.where(upper_side, lower, upper)
            piece = keep + swapped(give.astype(jnp.bfloat16), "section", bit).astype(give.dtype)
        for bit in range(bit_count):
            upper_side = section_index // 2**bit % 2 == 1
            other = swapped(piece, "section", bit)
            piece = jnp.where(
                upper_side,
                jnp.concatenate([other, piece], axis=1),
                jnp.concatenate([piece, other], axis=1),
            )
        return piece

    def apply_layer(stream, micro_index):
        routed_ids = routed_rows[micro_index, layer_index]
        live_count = routed_count[micro_index, layer_index]
        picked = jnp.take(stream, routed_ids, axis=0)
        floats = picked.astype(jnp.float32)
        squares_part = jnp.sum(floats * floats, axis=1)
        logit_part = jnp.sum(floats * router_row, axis=1)
        scaled = (floats * gain_row).astype(jnp.bfloat16)
        gate_part = jnp.dot(scaled, gate_block, preferred_element_type=jnp.float32)
        up_part = jnp.dot(scaled, up_block, preferred_element_type=jnp.float32)
        squares, logits = in_one((squares_part, logit_part), "tp")
        gate_cut, up_cut = in_one_piece((gate_part, up_part), "tp", 1, 0)
        inverse = lax.rsqrt(squares / D + EPSILON)[:, None]
        hidden = (jax.nn.silu(gate_cut * inverse) * (up_cut * inverse)).astype(jnp.bfloat16)
        partial_value = jnp.dot(
            gather_directly(hidden, "tp", 1), down_block, preferred_element_type=jnp.float32
        )
        output = sum_groups(partial_value)
        router_gate = jax.nn.sigmoid(logits)[:, None]
        updated = (floats + router_gate * output).astype(jnp.bfloat16)
        is_live = jnp.arange(capacity, dtype=jnp.int32) < live_count
        new_rows = jnp.where(is_live[:, None], updated, picked)
        return stream.at[routed_ids].set(new_rows)

    def advance(step_index, carried):
        passed, finished = carried
        incoming = shifted(passed, "section", group_size)
        micro_index = step_index - layer_index
        active = (micro_index >= 0) & (micro_index < micro_count)
        clipped = jnp.clip(micro_index, 0, micro_count - 1)
        entering = lax.dynamic_index_in_dim(tokens_in, clipped, 0, keepdims=False)
        current = jnp.where(layer_index == 0, entering, incoming)
        result = apply_layer(current, clipped)
        store_now = active & (layer_index == LAYERS - 1)
        stored = lax.dynamic_update_index_in_dim(finished, result, clipped, 0)
        finished = jnp.where(store_now, stored, finished)
        return (result, finished)

    starting = (
        jnp.zeros((token_count, quarter), jnp.bfloat16),
        jnp.zeros((micro_count, token_count, quarter), jnp.bfloat16),
    )
    last_pass, finished = lax.fori_loop(0, total_steps, advance, starting)
    owned_span = token_count // group_size
    position_in_group = section_index - (LAYERS - 1) * group_size
    owner = jnp.arange(token_count, dtype=jnp.int32) // owned_span
    mine = (owner == position_in_group) & (layer_index == LAYERS - 1)
    contribution = jnp.where(mine[None, :, None], finished.astype(jnp.float32), 0.0)
    gathered = sent_and_summed(contribution.astype(jnp.bfloat16), "section", 1)
    return gathered.astype(jnp.bfloat16)


def solution(mesh):
    return jax.shard_map(
        on_device,
        mesh=mesh,
        in_specs=(
            P(None, None, "tp"),
            P(None, "tp"),
            P(None, "tp"),
            P("section", "tp", None),
            P("section", "tp", None),
            P("section", None, "tp"),
            P(),
            P(),
        ),
        out_specs=P(None, "section", "tp"),
        check_vma=False,
    )
```

profile of v0, /device:TPU:1, one launch (start us, length us, event | category | flops | bytes accessed | tf_op | source)
XLA Modules:
  0.0 400.1 jit_solution(15126262746619735156)
XLA Ops:
  8.6 347.2 %while.19 = (s32[]{:T(128)}, bf16[224,1792]{1,0:T(8,128)(2,1)S(1)}, bf16[2,224,1792]{2,1,0:T(8,128)(2,1)}, pred[]{:T(512)}, s32[]{:T(128)}, /*index=5*/bf16[2,22...) while((s32[]{:T(128)}, bf16[224,1792]{1,0:T(8,128)(2,1)S(1)}, ...), condition=%wide.region_6.7_spmd, body=%wide.region_0.6_spmd.sunk | while | flops 1394484096 | bytes 76152504 | solution.py:156
  8.7 5.7 %collective-permute-start = (bf16[224,1792]{1,0:T(8,128)(2,1)S(1)}, bf16[224,1792]{1,0:T(8,128)(2,1)S(1)}, u32[]{:S(2)}, u32[]{:S(2)}) collective-permute-start(bf16[224,1792]{1,0:T(8,128)(2,1)S(1)} %get-tuple-element.1000), channel_id=1, source_target_pairs={{0,64},{4,68},{8,72},{12,76},{16,80},{20,84},{24,88},{28,92},{32,9... | collective-permute-start | bytes 2408456 | tf_op jit(solution)/shard_map/while/body/eval_jaxpr/ppermute | solution.py:57
  15.8 15.1 %collective-permute-done = bf16[224,1792]{1,0:T(8,128)(2,1)S(1)} collective-permute-done((bf16[224,1792]{1,0:T(8,128)(2,1)S(1)}, bf16[224,1792]{1,0:T(8,128)(2,1)S(1)}, u32[]{:S(2)}, u32[]{:S(2)}) %collective-permute-start) | collective-permute-done | bytes 802848 | tf_op jit(solution)/shard_map/while/body/eval_jaxpr/ppermute | solution.py:57
  39.2 9.0 %all_to_all.35 = f32[4,1,224]{2,1,0:T(1,128)S(1)} all-to-all(f32[4,1,224]{2,1,0:T(1,128)S(1)} %broadcast_in_dim.166), channel_id=1, replica_groups=mesh['section'=32,'tp'=4] {'tp'}, dimensions={0} | all-to-all | bytes 7168 | tf_op jit(solution)/shard_map/while/body/eval_jaxpr/all_to_all | solution.py:21
  48.3 17.5 %reduce-scatter.6.cloned.1.call-done = f32[288,224]{1,0:T(8,128)} async-done(((f32[1152,224]{1,0:T(8,128)}), f32[288,224]{1,0:T(8,128)}) %reduce-scatter.6.cloned.1.call-update) | async-done | bytes 258064 | tf_op jit(solution)/shard_map/while
  67.5 8.1 %all_to_all.36 = bf16[4,112,288]{1,2,0:T(8,128)(2,1)S(1)} all-to-all(bf16[4,112,288]{1,2,0:T(8,128)(2,1)S(1)} %broadcast_in_dim.167), channel_id=1, replica_groups=mesh['section'=32,'tp'=4] {'tp'}, dimensions={0} | all-to-all | bytes 516096 | tf_op jit(solution)/shard_map/while/body/eval_jaxpr/all_to_all | solution.py:21
  92.1 7.5 %collective-permute-start.4 = (bf16[112,112]{1,0:T(8,128)(2,1)S(1)}, bf16[112,112]{1,0:T(8,128)(2,1)S(1)}, u32[]{:S(2)}, u32[]{:S(2)}) collective-permute-start(bf16[112,112]{1,0:T(8,128)(2,1)S(1)} %select_convert_fusion.12), channel_id=1, source_target_pairs={{0,4},{4,0},{8,12},{12,8},{16,20},{20,16},{24,28},{28,24},{32,36},... | collective-permute-start | bytes 75272 | tf_op jit(solution)/shard_map/while/body/eval_jaxpr/ppermute | solution.py:16
  109.1 5.1 %collective-permute-done.7 = f32[112,448]{1,0:T(8,128)S(1)} collective-permute-done((f32[112,448]{1,0:T(8,128)S(1)}, f32[112,448]{1,0:T(8,128)S(1)}, u32[]{:S(2)}, u32[]{:S(2)}) %collective-permute-start.7) | collective-permute-done | bytes 200736 | tf_op jit(solution)/shard_map/while/body/eval_jaxpr/ppermute | solution.py:16
  117.1 6.3 %collective-permute-done.8 = f32[112,896]{1,0:T(8,128)} collective-permute-done((f32[112,896]{1,0:T(8,128)S(1)}, f32[112,896]{1,0:T(8,128)}, u32[]{:S(2)}, u32[]{:S(2)}) %collective-permute-start.8) | collective-permute-done | bytes 401440 | tf_op jit(solution)/shard_map/while/body/eval_jaxpr/ppermute | solution.py:16
  133.3 12.8 %collective-permute-done = bf16[224,1792]{1,0:T(8,128)(2,1)S(1)} collective-permute-done((bf16[224,1792]{1,0:T(8,128)(2,1)S(1)}, bf16[224,1792]{1,0:T(8,128)(2,1)S(1)}, u32[]{:S(2)}, u32[]{:S(2)}) %collective-permute-start) | collective-permute-done | bytes 802848 | tf_op jit(solution)/shard_map/while/body/eval_jaxpr/ppermute | solution.py:57
  154.5 6.5 %all_to_all.35 = f32[4,1,224]{2,1,0:T(1,128)S(1)} all-to-all(f32[4,1,224]{2,1,0:T(1,128)S(1)} %broadcast_in_dim.166), channel_id=1, replica_groups=mesh['section'=32,'tp'=4] {'tp'}, dimensions={0} | all-to-all | bytes 7168 | tf_op jit(solution)/shard_map/while/body/eval_jaxpr/all_to_all | solution.py:21
  161.1 19.0 %reduce-scatter.6.cloned.1.call-done = f32[288,224]{1,0:T(8,128)} async-done(((f32[1152,224]{1,0:T(8,128)}), f32[288,224]{1,0:T(8,128)}) %reduce-scatter.6.cloned.1.call-update) | async-done | bytes 258064 | tf_op jit(solution)/shard_map/while
  181.8 8.1 %all_to_all.36 = bf16[4,112,288]{1,2,0:T(8,128)(2,1)S(1)} all-to-all(bf16[4,112,288]{1,2,0:T(8,128)(2,1)S(1)} %broadcast_in_dim.167), channel_id=1, replica_groups=mesh['section'=32,'tp'=4] {'tp'}, dimensions={0} | all-to-all | bytes 516096 | tf_op jit(solution)/shard_map/while/body/eval_jaxpr/all_to_all | solution.py:21
  206.4 7.5 %collective-permute-start.4 = (bf16[112,112]{1,0:T(8,128)(2,1)S(1)}, bf16[112,112]{1,0:T(8,128)(2,1)S(1)}, u32[]{:S(2)}, u32[]{:S(2)}) collective-permute-start(bf16[112,112]{1,0:T(8,128)(2,1)S(1)} %select_convert_fusion.12), channel_id=1, source_target_pairs={{0,4},{4,0},{8,12},{12,8},{16,20},{20,16},{24,28},{28,24},{32,36},... | collective-permute-start | bytes 75272 | tf_op jit(solution)/shard_map/while/body/eval_jaxpr/ppermute | solution.py:16
  223.4 5.2 %collective-permute-done.7 = f32[112,448]{1,0:T(8,128)S(1)} collective-permute-done((f32[112,448]{1,0:T(8,128)S(1)}, f32[112,448]{1,0:T(8,128)S(1)}, u32[]{:S(2)}, u32[]{:S(2)}) %collective-permute-start.7) | collective-permute-done | bytes 200736 | tf_op jit(solution)/shard_map/while/body/eval_jaxpr/ppermute | solution.py:16
  231.3 6.4 %collective-permute-done.8 = f32[112,896]{1,0:T(8,128)} collective-permute-done((f32[112,896]{1,0:T(8,128)S(1)}, f32[112,896]{1,0:T(8,128)}, u32[]{:S(2)}, u32[]{:S(2)}) %collective-permute-start.8) | collective-permute-done | bytes 401440 | tf_op jit(solution)/shard_map/while/body/eval_jaxpr/ppermute | solution.py:16
  247.7 12.8 %collective-permute-done = bf16[224,1792]{1,0:T(8,128)(2,1)S(1)} collective-permute-done((bf16[224,1792]{1,0:T(8,128)(2,1)S(1)}, bf16[224,1792]{1,0:T(8,128)(2,1)S(1)}, u32[]{:S(2)}, u32[]{:S(2)}) %collective-permute-start) | collective-permute-done | bytes 802848 | tf_op jit(solution)/shard_map/while/body/eval_jaxpr/ppermute | solution.py:57
  268.8 6.5 %all_to_all.35 = f32[4,1,224]{2,1,0:T(1,128)S(1)} all-to-all(f32[4,1,224]{2,1,0:T(1,128)S(1)} %broadcast_in_dim.166), channel_id=1, replica_groups=mesh['section'=32,'tp'=4] {'tp'}, dimensions={0} | all-to-all | bytes 7168 | tf_op jit(solution)/shard_map/while/body/eval_jaxpr/all_to_all | solution.py:21
  275.4 18.5 %reduce-scatter.6.cloned.1.call-done = f32[288,224]{1,0:T(8,128)} async-done(((f32[1152,224]{1,0:T(8,128)}), f32[288,224]{1,0:T(8,128)}) %reduce-scatter.6.cloned.1.call-update) | async-done | bytes 258064 | tf_op jit(solution)/shard_map/while
  295.6 8.2 %all_to_all.36 = bf16[4,112,288]{1,2,0:T(8,128)(2,1)S(1)} all-to-all(bf16[4,112,288]{1,2,0:T(8,128)(2,1)S(1)} %broadcast_in_dim.167), channel_id=1, replica_groups=mesh['section'=32,'tp'=4] {'tp'}, dimensions={0} | all-to-all | bytes 516096 | tf_op jit(solution)/shard_map/while/body/eval_jaxpr/all_to_all | solution.py:21
  320.4 7.8 %collective-permute-start.4 = (bf16[112,112]{1,0:T(8,128)(2,1)S(1)}, bf16[112,112]{1,0:T(8,128)(2,1)S(1)}, u32[]{:S(2)}, u32[]{:S(2)}) collective-permute-start(bf16[112,112]{1,0:T(8,128)(2,1)S(1)} %select_convert_fusion.12), channel_id=1, source_target_pairs={{0,4},{4,0},{8,12},{12,8},{16,20},{20,16},{24,28},{28,24},{32,36},... | collective-permute-start | bytes 75272 | tf_op jit(solution)/shard_map/while/body/eval_jaxpr/ppermute | solution.py:16
  337.6 5.2 %collective-permute-done.7 = f32[112,448]{1,0:T(8,128)S(1)} collective-permute-done((f32[112,448]{1,0:T(8,128)S(1)}, f32[112,448]{1,0:T(8,128)S(1)}, u32[]{:S(2)}, u32[]{:S(2)}) %collective-permute-start.7) | collective-permute-done | bytes 200736 | tf_op jit(solution)/shard_map/while/body/eval_jaxpr/ppermute | solution.py:16
  345.4 6.5 %collective-permute-done.8 = f32[112,896]{1,0:T(8,128)} collective-permute-done((f32[112,896]{1,0:T(8,128)S(1)}, f32[112,896]{1,0:T(8,128)}, u32[]{:S(2)}, u32[]{:S(2)}) %collective-permute-start.8) | collective-permute-done | bytes 401440 | tf_op jit(solution)/shard_map/while/body/eval_jaxpr/ppermute | solution.py:16
  359.4 32.1 %all_to_all.34 = bf16[32,2,7,1792]{3,1,2,0:T(2,128)(2,1)S(1)} all-to-all(bf16[32,2,7,1792]{3,1,2,0:T(2,128)(2,1)S(1)} %bitcast.60), channel_id=1, replica_groups=mesh['section'=32,'tp'=4] {'section'}, dimensions={0} | all-to-all | bytes 3211264 | tf_op jit(solution)/shard_map/all_to_all | solution.py:68
  (192 shorter events, 148.9 us)
Async XLA Ops:
  8.7 57.1 %reduce-scatter.6.cloned.1.call-start = ((), (), s32[]{:S(2)}) async-start(), calls=%async_computation.4 | async-start | bytes 1474560 | tf_op jit(solution)/shard_map/while
  8.7 22.2 %collective-permute-start = (bf16[224,1792]{1,0:T(8,128)(2,1)S(1)}, bf16[224,1792]{1,0:T(8,128)(2,1)S(1)}, u32[]{:S(2)}, u32[]{:S(2)}) collective-permute-start(bf16[224,1792]{1,0:T(8,128)(2,1)S(1)} %get-tuple-element.1000), channel_id=1, source_target_pairs={{0,64},{4,68},{8,72},{12,76},{16,80},{20,84},{24,88},{28,92},{32,9... | collective-permute-start | bytes 2408456 | tf_op jit(solution)/shard_map/while/body/eval_jaxpr/ppermute | solution.py:57
  78.6 4.6 %collective-permute-start.1 = (bf16[112,896]{1,0:T(8,128)(2,1)S(1)}, bf16[112,896]{1,0:T(8,128)(2,1)S(1)}, u32[]{:S(2)}, u32[]{:S(2)}) collective-permute-start(bf16[112,896]{1,0:T(8,128)(2,1)S(1)} %select_convert_fusion.9), channel_id=1, source_target_pairs={{0,32},{4,36},{8,40},{12,44},{16,48},{20,52},{24,56},{28,60},{32,0... | collective-permute-start | bytes 602120 | tf_op jit(solution)/shard_map/while/body/eval_jaxpr/ppermute | solution.py:16
  83.4 5.2 %collective-permute-start.2 = (bf16[112,448]{1,0:T(8,128)(2,1)S(1)}, bf16[112,448]{1,0:T(8,128)(2,1)S(1)}, u32[]{:S(2)}, u32[]{:S(2)}) collective-permute-start(bf16[112,448]{1,0:T(8,128)(2,1)S(1)} %select_convert_fusion.10), channel_id=1, source_target_pairs={{0,16},{4,20},{8,24},{12,28},{16,0},{20,4},{24,8},{28,12},{32,48},... | collective-permute-start | bytes 301064 | tf_op jit(solution)/shard_map/while/body/eval_jaxpr/ppermute | solution.py:16
  92.1 8.4 %collective-permute-start.4 = (bf16[112,112]{1,0:T(8,128)(2,1)S(1)}, bf16[112,112]{1,0:T(8,128)(2,1)S(1)}, u32[]{:S(2)}, u32[]{:S(2)}) collective-permute-start(bf16[112,112]{1,0:T(8,128)(2,1)S(1)} %select_convert_fusion.12), channel_id=1, source_target_pairs={{0,4},{4,0},{8,12},{12,8},{16,20},{20,16},{24,28},{28,24},{32,36},... | collective-permute-start | bytes 75272 | tf_op jit(solution)/shard_map/while/body/eval_jaxpr/ppermute | solution.py:16
  102.1 4.4 %collective-permute-start.6 = (f32[112,224]{1,0:T(8,128)S(1)}, f32[112,224]{1,0:T(8,128)S(1)}, u32[]{:S(2)}, u32[]{:S(2)}) collective-permute-start(f32[112,224]{1,0:T(8,128)S(1)} %maximum_select_fusion.7), channel_id=1, source_target_pairs={{0,8},{4,12},{8,0},{12,4},{16,24},{20,28},{24,16},{28,20},{32,40},... | collective-permute-start | bytes 301064 | tf_op jit(solution)/shard_map/while/body/eval_jaxpr/ppermute | solution.py:16
  106.7 7.5 %collective-permute-start.7 = (f32[112,448]{1,0:T(8,128)S(1)}, f32[112,448]{1,0:T(8,128)S(1)}, u32[]{:S(2)}, u32[]{:S(2)}) collective-permute-start(f32[112,448]{1,0:T(8,128)S(1)} %maximum_select_fusion.8), channel_id=1, source_target_pairs={{0,16},{4,20},{8,24},{12,28},{16,0},{20,4},{24,8},{28,12},{32,48},... | collective-permute-start | bytes 602120 | tf_op jit(solution)/shard_map/while/body/eval_jaxpr/ppermute | solution.py:16
  114.4 9.0 %collective-permute-start.8 = (f32[112,896]{1,0:T(8,128)S(1)}, f32[112,896]{1,0:T(8,128)}, u32[]{:S(2)}, u32[]{:S(2)}) collective-permute-start(f32[112,896]{1,0:T(8,128)S(1)} %maximum_select_fusion.9), channel_id=1, source_target_pairs={{0,32},{4,36},{8,40},{12,44},{16,48},{20,52},{24,56},{28,60},{32,0... | collective-permute-start | bytes 1204232 | tf_op jit(solution)/shard_map/while/body/eval_jaxpr/ppermute | solution.py:16
  127.2 52.8 %reduce-scatter.6.cloned.1.call-start = ((), (), s32[]{:S(2)}) async-start(), calls=%async_computation.4 | async-start | bytes 1474560 | tf_op jit(solution)/shard_map/while
  127.2 18.9 %collective-permute-start = (bf16[224,1792]{1,0:T(8,128)(2,1)S(1)}, bf16[224,1792]{1,0:T(8,128)(2,1)S(1)}, u32[]{:S(2)}, u32[]{:S(2)}) collective-permute-start(bf16[224,1792]{1,0:T(8,128)(2,1)S(1)} %get-tuple-element.1000), channel_id=1, source_target_pairs={{0,64},{4,68},{8,72},{12,76},{16,80},{20,84},{24,88},{28,92},{32,9... | collective-permute-start | bytes 2408456 | tf_op jit(solution)/shard_map/while/body/eval_jaxpr/ppermute | solution.py:57
  192.9 4.6 %collective-permute-start.1 = (bf16[112,896]{1,0:T(8,128)(2,1)S(1)}, bf16[112,896]{1,0:T(8,128)(2,1)S(1)}, u32[]{:S(2)}, u32[]{:S(2)}) collective-permute-start(bf16[112,896]{1,0:T(8,128)(2,1)S(1)} %select_convert_fusion.9), channel_id=1, source_target_pairs={{0,32},{4,36},{8,40},{12,44},{16,48},{20,52},{24,56},{28,60},{32,0... | collective-permute-start | bytes 602120 | tf_op jit(solution)/shard_map/while/body/eval_jaxpr/ppermute | solution.py:16
  197.7 5.2 %collective-permute-start.2 = (bf16[112,448]{1,0:T(8,128)(2,1)S(1)}, bf16[112,448]{1,0:T(8,128)(2,1)S(1)}, u32[]{:S(2)}, u32[]{:S(2)}) collective-permute-start(bf16[112,448]{1,0:T(8,128)(2,1)S(1)} %select_convert_fusion.10), channel_id=1, source_target_pairs={{0,16},{4,20},{8,24},{12,28},{16,0},{20,4},{24,8},{28,12},{32,48},... | collective-permute-start | bytes 301064 | tf_op jit(solution)/shard_map/while/body/eval_jaxpr/ppermute | solution.py:16
  206.4 8.4 %collective-permute-start.4 = (bf16[112,112]{1,0:T(8,128)(2,1)S(1)}, bf16[112,112]{1,0:T(8,128)(2,1)S(1)}, u32[]{:S(2)}, u32[]{:S(2)}) collective-permute-start(bf16[112,112]{1,0:T(8,128)(2,1)S(1)} %select_convert_fusion.12), channel_id=1, source_target_pairs={{0,4},{4,0},{8,12},{12,8},{16,20},{20,16},{24,28},{28,24},{32,36},... | collective-permute-start | bytes 75272 | tf_op jit(solution)/shard_map/while/body/eval_jaxpr/ppermute | solution.py:16
  216.4 4.4 %collective-permute-start.6 = (f32[112,224]{1,0:T(8,128)S(1)}, f32[112,224]{1,0:T(8,128)S(1)}, u32[]{:S(2)}, u32[]{:S(2)}) collective-permute-start(f32[112,224]{1,0:T(8,128)S(1)} %maximum_select_fusion.7), channel_id=1, source_target_pairs={{0,8},{4,12},{8,0},{12,4},{16,24},{20,28},{24,16},{28,20},{32,40},... | collective-permute-start | bytes 301064 | tf_op jit(solution)/shard_map/while/body/eval_jaxpr/ppermute | solution.py:16
  221.0 7.5 %collective-permute-start.7 = (f32[112,448]{1,0:T(8,128)S(1)}, f32[112,448]{1,0:T(8,128)S(1)}, u32[]{:S(2)}, u32[]{:S(2)}) collective-permute-start(f32[112,448]{1,0:T(8,128)S(1)} %maximum_select_fusion.8), channel_id=1, source_target_pairs={{0,16},{4,20},{8,24},{12,28},{16,0},{20,4},{24,8},{28,12},{32,48},... | collective-permute-start | bytes 602120 | tf_op jit(solution)/shard_map/while/body/eval_jaxpr/ppermute | solution.py:16
  228.7 9.0 %collective-permute-start.8 = (f32[112,896]{1,0:T(8,128)S(1)}, f32[112,896]{1,0:T(8,128)}, u32[]{:S(2)}, u32[]{:S(2)}) collective-permute-start(f32[112,896]{1,0:T(8,128)S(1)} %maximum_select_fusion.9), channel_id=1, source_target_pairs={{0,32},{4,36},{8,40},{12,44},{16,48},{20,52},{24,56},{28,60},{32,0... | collective-permute-start | bytes 1204232 | tf_op jit(solution)/shard_map/while/body/eval_jaxpr/ppermute | solution.py:16
  241.6 52.3 %reduce-scatter.6.cloned.1.call-start = ((), (), s32[]{:S(2)}) async-start(), calls=%async_computation.4 | async-start | bytes 1474560 | tf_op jit(solution)/shard_map/while
  241.6 18.9 %collective-permute-start = (bf16[224,1792]{1,0:T(8,128)(2,1)S(1)}, bf16[224,1792]{1,0:T(8,128)(2,1)S(1)}, u32[]{:S(2)}, u32[]{:S(2)}) collective-permute-start(bf16[224,1792]{1,0:T(8,128)(2,1)S(1)} %get-tuple-element.1000), channel_id=1, source_target_pairs={{0,64},{4,68},{8,72},{12,76},{16,80},{20,84},{24,88},{28,92},{32,9... | collective-permute-start | bytes 2408456 | tf_op jit(solution)/shard_map/while/body/eval_jaxpr/ppermute | solution.py:57
  306.9 4.7 %collective-permute-start.1 = (bf16[112,896]{1,0:T(8,128)(2,1)S(1)}, bf16[112,896]{1,0:T(8,128)(2,1)S(1)}, u32[]{:S(2)}, u32[]{:S(2)}) collective-permute-start(bf16[112,896]{1,0:T(8,128)(2,1)S(1)} %select_convert_fusion.9), channel_id=1, source_target_pairs={{0,32},{4,36},{8,40},{12,44},{16,48},{20,52},{24,56},{28,60},{32,0... | collective-permute-start | bytes 602120 | tf_op jit(solution)/shard_map/while/body/eval_jaxpr/ppermute | solution.py:16
  311.7 5.2 %collective-permute-start.2 = (bf16[112,448]{1,0:T(8,128)(2,1)S(1)}, bf16[112,448]{1,0:T(8,128)(2,1)S(1)}, u32[]{:S(2)}, u32[]{:S(2)}) collective-permute-start(bf16[112,448]{1,0:T(8,128)(2,1)S(1)} %select_convert_fusion.10), channel_id=1, source_target_pairs={{0,16},{4,20},{8,24},{12,28},{16,0},{20,4},{24,8},{28,12},{32,48},... | collective-permute-start | bytes 301064 | tf_op jit(solution)/shard_map/while/body/eval_jaxpr/ppermute | solution.py:16
  320.4 8.7 %collective-permute-start.4 = (bf16[112,112]{1,0:T(8,128)(2,1)S(1)}, bf16[112,112]{1,0:T(8,128)(2,1)S(1)}, u32[]{:S(2)}, u32[]{:S(2)}) collective-permute-start(bf16[112,112]{1,0:T(8,128)(2,1)S(1)} %select_convert_fusion.12), channel_id=1, source_target_pairs={{0,4},{4,0},{8,12},{12,8},{16,20},{20,16},{24,28},{28,24},{32,36},... | collective-permute-start | bytes 75272 | tf_op jit(solution)/shard_map/while/body/eval_jaxpr/ppermute | solution.py:16
  330.7 4.4 %collective-permute-start.6 = (f32[112,224]{1,0:T(8,128)S(1)}, f32[112,224]{1,0:T(8,128)S(1)}, u32[]{:S(2)}, u32[]{:S(2)}) collective-permute-start(f32[112,224]{1,0:T(8,128)S(1)} %maximum_select_fusion.7), channel_id=1, source_target_pairs={{0,8},{4,12},{8,0},{12,4},{16,24},{20,28},{24,16},{28,20},{32,40},... | collective-permute-start | bytes 301064 | tf_op jit(solution)/shard_map/while/body/eval_jaxpr/ppermute | solution.py:16
  335.3 7.5 %collective-permute-start.7 = (f32[112,448]{1,0:T(8,128)S(1)}, f32[112,448]{1,0:T(8,128)S(1)}, u32[]{:S(2)}, u32[]{:S(2)}) collective-permute-start(f32[112,448]{1,0:T(8,128)S(1)} %maximum_select_fusion.8), channel_id=1, source_target_pairs={{0,16},{4,20},{8,24},{12,28},{16,0},{20,4},{24,8},{28,12},{32,48},... | collective-permute-start | bytes 602120 | tf_op jit(solution)/shard_map/while/body/eval_jaxpr/ppermute | solution.py:16
  343.0 9.0 %collective-permute-start.8 = (f32[112,896]{1,0:T(8,128)S(1)}, f32[112,896]{1,0:T(8,128)}, u32[]{:S(2)}, u32[]{:S(2)}) collective-permute-start(f32[112,896]{1,0:T(8,128)S(1)} %maximum_select_fusion.9), channel_id=1, source_target_pairs={{0,32},{4,36},{8,40},{12,44},{16,48},{20,52},{24,56},{28,60},{32,0... | collective-permute-start | bytes 1204232 | tf_op jit(solution)/shard_map/while/body/eval_jaxpr/ppermute | solution.py:16
  (18 other events, 280.9 us)
Sparse Core Ops, SparseCore 0:
  38.9 26.8 reduce-scatter.5
  154.2 25.8 reduce-scatter.5
  268.5 25.3 reduce-scatter.5
where the time goes:
time: 401 us; the launch traced here: 400 us
  waiting for transfers between devices  170 us (42%)
  blocking collectives  78.4 us (20%)
  starting transfers between devices  68.5 us (17%)
  other arithmetic  27.4 us (7%)
  local copies, waits for them, and re-layouts  21.4 us (5%)
  matrix products  20.9 us (5%)
  between operations  13.1 us (3%)
    ppermute x24, waiting for transfers between devices, swapped(): return lax.ppermute(value, axis, pairs)  73.8 us
    while x6, waiting for transfers between devices  55.1 us
    ppermute x24, starting transfers between devices, swapped(): return lax.ppermute(value, axis, pairs)  53.5 us
    all_to_all x6, blocking collectives, from_everyone(): return lax.all_to_all(copies, axis, split_axis=0, concat_axis=0, tiled=True)  46.2 us
    ppermute x3, waiting for transfers between devices, shifted(): return lax.ppermute(value, axis, pairs)  40.8 us
    all_to_all x1, blocking collectives, sent_and_summed(): lax.all_to_all(blocks, axis, split_axis=0, concat_axis=0, tiled=True)  32.1 us
    ppermute x3, starting transfers between devices, shifted(): return lax.ppermute(value, axis, pairs)  15 us
    dot_general x3, matrix products, apply_layer(): gate_part = jnp.dot(scaled, gate_block, preferred_element_type=jnp.float32)  9.46 us
  transfers between devices with their start and end apart: 30, of which 30 were waited for; matrix products, arithmetic and copies ran while one was open for 2% of the time, Pallas kernels for 0%

commit v1 on v0

v1 whole, which is shorter than its diff:
```python
import jax
import jax.numpy as jnp
from jax import lax
from jax.experimental import pallas as pl
from jax.experimental.pallas import tpu as pltpu
from jax.sharding import PartitionSpec as P

MESH = pl.DeviceIdType.MESH
F32 = jnp.float32
BF16 = jnp.bfloat16

MICRO = 2
CAP = 112
TOK = 224
Q = 1792
HID = 1152
D = 7168
EPSILON = 1e-06
ROWS = 128
HALF = Q // 2
BLOCKS = HALF // 128
OWN_TOKENS = 7
CHUNKS = ((0, 512), (512, 640))


def iota(shape, dim):
    return lax.broadcasted_iota(jnp.int32, shape, dim)


def onehot(hit):
    return jnp.where(hit, 1.0, 0.0).astype(BF16)


def padded_column(row, fill):
    r, c = iota((ROWS, CAP), 0), iota((ROWS, CAP), 1)
    hit = (c == r - 4 * (r >> 5)) & ((r & 31) < 28)
    column = jnp.sum(jnp.where(hit, row, 0.0), axis=1, keepdims=True)
    return jnp.where((iota((ROWS, 1), 0) & 31) < 28, column, fill)


def as_row(column):
    n = column.shape[0]
    eye = iota((n, n), 0) == iota((n, n), 1)
    return jnp.sum(jnp.where(eye, column, 0.0), axis=0, keepdims=True)


def as_column(row, first, n):
    hit = iota((n, ROWS), 1) == iota((n, ROWS), 0) + first
    return jnp.sum(jnp.where(hit, row, 0.0), axis=1, keepdims=True)


def dot(a, b):
    return jnp.dot(a, b, preferred_element_type=F32)


def body(
    tok_h, gain_h, router_h, wg_h, wu_h, wd_h, rows_h, cnt_h,
    out_ref,
    tok, gain, router, wg, wu, wd, rows, cnt,
    picked, scaled, stat, stat_in, part, relay, ring, back, hidden, xcore, xcore_in, keep,
    summed, summed_in, updated, blocks, final, ready, final_in,
    load_sem, stat_s, stat_r, relay_s, relay_r, ring_s, ring_r, back_s, back_r, hid_s, hid_r,
    core_s, core_r, sum_s, sum_r, hop_s, blk_s, fwd_s, blk_r, fin_s, fin_r,
):
    sec = lax.axis_index("section")
    tp = lax.axis_index("tp")
    core = lax.rem(sec, 2)
    group = sec // 16
    chip = lax.rem(sec, 16) // 2
    ahead = lax.rem(tp + 1 + 2 * core, 4)
    behind = lax.rem(tp + 3 + 2 * core, 4)
    across = lax.rem(tp + 2, 4)
    sibling = sec + 1 - 2 * core
    sections, tps = 32, 4

    barrier = pltpu.get_barrier_semaphore()

    @pl.loop(1, sections)
    def _(k):
        pl.semaphore_signal(
            barrier, inc=1, device_id={"section": lax.rem(sec + k, sections), "tp": tp}, device_id_type=MESH
        )

    for k in range(1, tps):
        pl.semaphore_signal(
            barrier, inc=1, device_id={"section": sec, "tp": lax.rem(tp + k, tps)}, device_id_type=MESH
        )

    loads = []

    def load(src, dst):
        copy = pltpu.make_async_copy(src, dst, load_sem.at[len(loads)])
        copy.start()
        loads.append(copy)
        return copy

    small = [load(rows_h, rows), load(cnt_h, cnt), load(gain_h, gain), load(router_h, router)]
    tok_load = [load(tok_h.at[m], tok.at[m]) for m in range(MICRO)]
    wgu_load = []
    for start, n in CHUNKS:
        cols = pl.ds(start, n)
        wgu_load.append(
            (load(wg_h.at[0, :, cols], wg.at[:, cols]), load(wu_h.at[0, :, cols], wu.at[:, cols]))
        )
    wd_load = load(wd_h.at[0], wd)

    sends = []

    def remote(src, dst, ss, rs, section=None, z=None):
        return pltpu.make_async_remote_copy(
            src_ref=src,
            dst_ref=dst,
            send_sem=ss,
            recv_sem=rs,
            device_id={"section": sec if section is None else section, "tp": tp if z is None else z},
            device_id_type=MESH,
        )

    def send(copy):
        copy.start()
        sends.append((None, copy))

    def routed(m, k):
        ids = rows[m, k : k + 1, :].astype(F32)
        count = cnt[m : m + 1, k : k + 1]
        return ids, iota((1, CAP), 1) < count

    def pick(m):
        for copy in small if m == 0 else []:
            copy.wait()
        tok_load[m].wait()

        @pl.when(group == 0)
        def _():
            ids, _ = routed(m, 0)
            column = padded_column(ids, -1.0)
            old = onehot(column == iota((ROWS, TOK), 1).astype(F32))
            for b in range(Q // 256):
                cols = pl.ds(256 * b, 256)
                picked[m, :, cols] = dot(old, tok[m, :, cols]).astype(BF16)

        @pl.when(group == 1)
        def _():
            ids1, _ = routed(m, 1)
            column = padded_column(ids1, -1.0)
            ids0, live0 = routed(m, 0)
            row0 = as_row(padded_column(jnp.where(live0, ids0, -2.0), -2.0))
            hit = column == row0
            is_new = jnp.sum(jnp.where(hit, 1.0, 0.0), axis=1, keepdims=True) > 0.5
            new = onehot(hit)
            old = onehot((column == iota((ROWS, TOK), 1).astype(F32)) & ~is_new)
            for b in range(2 * BLOCKS):
                cols = pl.ds(128 * b, 128)
                picked[m, :, cols] = (dot(old, tok[m, :, cols]) + dot(new, blocks[m, b])).astype(BF16)

        squares = jnp.zeros((ROWS, 256), F32)
        logits = jnp.zeros((ROWS, 256), F32)
        for b in range(Q // 256):
            cols = pl.ds(256 * b, 256)
            values = picked[m, :, cols].astype(F32)
            squares = squares + values * values
            logits = logits + values * router[pl.ds(group, 1), cols]
            scaled[m, :, cols] = (values * gain[pl.ds(group, 1), cols]).astype(BF16)
        squares = as_row(jnp.sum(squares, axis=1, keepdims=True))
        logits = as_row(jnp.sum(logits, axis=1, keepdims=True))
        which = iota((8, ROWS), 0)
        stat[m] = jnp.where(which == 0, squares, jnp.where(which == 1, logits, 0.0))

    def stat_copy(m, k):
        return remote(stat.at[m], stat_in.at[m, k - 1], stat_s.at[m, k - 1], stat_r.at[m, k - 1], z=lax.rem(tp + k, tps))

    def send_stats(m):
        for k in range(1, tps):
            send(stat_copy(m, k))

    def spans(n):
        start, width = CHUNKS[n]
        return pl.ds(2 * start, 2 * width), 2 * start, width

    def relay_copy(m, n):
        cols = spans(n)[0]
        return remote(part.at[m, across, :, cols], relay.at[m, :, cols], relay_s.at[m, n], relay_r.at[m, n], z=ahead)

    def back_copy(m, n):
        cols = spans(n)[0]
        return remote(part.at[m, behind, :, cols], back.at[m, :, cols], back_s.at[m, n], back_r.at[m, n], z=behind)

    def ring_copy(m, n):
        cols = spans(n)[0]
        return remote(ring.at[m, 0, :, cols], ring.at[m, 1, :, cols], ring_s.at[m, n], ring_r.at[m, n], z=ahead)

    def project(m, n):
        start, width = CHUNKS[n]
        if m == 0:
            wgu_load[n][0].wait()
        x = scaled[m]
        gate = dot(x, wg[:, start : start + width]).astype(BF16)
        part[m, :, :, 2 * start : 2 * start + width] = gate.reshape(tps, 32, width)
        if m == 0:
            wgu_load[n][1].wait()
        up = dot(x, wu[:, start : start + width]).astype(BF16)
        part[m, :, :, 2 * start + width : 2 * start + 2 * width] = up.reshape(tps, 32, width)
        if n == 0:
            send_stats(m)
        send(relay_copy(m, n))
        send(back_copy(m, n))

    def pass_on(m, n):
        cols = spans(n)[0]
        relay_copy(m, n).wait_recv()
        ring[m, 0, :, cols] = (part[m, ahead, :, cols].astype(F32) + relay[m, :, cols].astype(F32)).astype(BF16)
        send(ring_copy(m, n))

    def total_stats(m):
        return stat[m] + stat_in[m, 0] + stat_in[m, 1] + stat_in[m, 2]

    def hidden_copy(m, n, k):
        start, width = CHUNKS[n]
        mine = hidden.at[m, tp, :, pl.ds(start, width)]
        return remote(mine, mine, hid_s.at[m, n, k - 1], hid_r.at[m, n, k - 1], z=lax.rem(tp + k, tps))

    def activate(m, n):
        cols, first, width = spans(n)
        start = CHUNKS[n][0]
        if n == 0:
            for k in range(1, tps):
                stat_copy(m, k).wait_recv()
        back_copy(m, n).wait_recv()
        ring_copy(m, n).wait_recv()
        inverse = lax.rsqrt(as_column(total_stats(m)[0:1], 32 * tp, 32) / D + EPSILON)

        def values(at):
            c = pl.ds(at, width)
            return part[m, tp, :, c].astype(F32) + back[m, :, c].astype(F32) + ring[m, 1, :, c].astype(F32)

        gate = values(first) * inverse
        up = values(first + width) * inverse
        hidden[m, tp, :, start : start + width] = (gate / (1.0 + jnp.exp(-gate)) * up).astype(BF16)
        for k in (2, 1, 3):
            send(hidden_copy(m, n, k))

    def core_copy(m):
        return remote(xcore.at[m], xcore_in.at[m], core_s.at[m], core_r.at[m], section=sibling)

    def down(m):
        for n in range(len(CHUNKS)):
            for k in range(1, tps):
                hidden_copy(m, n, k).wait_recv()
        if m == 0:
            wd_load.wait()
        x = hidden[m].reshape(ROWS, HID)
        theirs = pl.ds(pl.multiple_of(HALF * (1 - core), 128), HALF)
        xcore[m] = dot(x, wd[:, theirs]).astype(BF16)
        send(core_copy(m))
        mine = pl.ds(pl.multiple_of(HALF * core, 128), HALF)
        keep[m] = dot(x, wd[:, mine])

    def sum_copy(m, k):
        there = lax.rem(chip + k, 8)
        return there < BLOCKS, remote(
            summed.at[m, there], summed_in.at[m, k - 1], sum_s.at[m, k - 1], sum_r.at[m, k - 1],
            section=16 * group + 2 * there + core,
        )

    def send_if(condition, copy):
        @pl.when(condition)
        def _():
            copy.start()

        sends.append((condition, copy))

    def spread(m):
        core_copy(m).wait_recv()
        for b in range(BLOCKS):
            cols = pl.ds(128 * b, 128)
            summed[m, b] = (keep[m, :, cols] + xcore_in[m, :, cols].astype(F32)).astype(BF16)
        for k in range(1, 8):
            there = lax.rem(chip + k, 8)

            @pl.when(there < BLOCKS)
            def _():
                sum_copy(m, k)[1].start()

            sends.append((there < BLOCKS, sum_copy(m, k)[1]))

    owner = chip < BLOCKS
    my_block = BLOCKS * core + chip
    my_columns = pl.ds(pl.multiple_of(128 * jnp.minimum(my_block, 2 * BLOCKS - 1), 128), 128)

    def hop_copy(m):
        return remote(
            updated.at[m], blocks.at[m, my_block], hop_s.at[m], blk_r.at[m, my_block],
            section=16 + 2 * lax.rem(chip + 4, 8) + core,
        )

    def combine(m):
        @pl.when(owner)
        def _():
            total = summed[m, chip].astype(F32)
            for k in range(1, 8):
                sum_copy(m, k)[1].wait_recv()
                total = total + summed_in[m, k - 1].astype(F32)
            logits = as_column(total_stats(m)[1:2], 0, ROWS)
            gate = 1.0 / (1.0 + jnp.exp(-logits))
            updated[m] = (picked[m, :, my_columns].astype(F32) + gate * total).astype(BF16)

            @pl.when(group == 0)
            def _():
                hop_copy(m).start()

        sends.append((owner & (group == 0), hop_copy(m)))

    source = lax.rem(chip + 4, 8)
    has_block = source < BLOCKS

    def block_copy(m, k):
        block = BLOCKS * core + source
        return remote(
            blocks.at[m, block], blocks.at[m, block], blk_s.at[m, k - 1], blk_r.at[m, block],
            section=16 + 2 * lax.rem(chip + k, 8) + core,
        )

    def forward_copy(m, k):
        block = BLOCKS * core + lax.rem(source + k, 8)
        return remote(
            blocks.at[m, block], blocks.at[m, block], fwd_s.at[m, k], blk_r.at[m, block], section=sibling
        )

    def arrival(m, block):
        return remote(blocks.at[m, block], blocks.at[m, block], fwd_s.at[m, 0], blk_r.at[m, block], section=sibling)

    def broadcast(m):
        @pl.when((group == 1) & has_block)
        def _():
            arrival(m, BLOCKS * core + source).wait_recv()
            for k in range(1, 8):
                block_copy(m, k).start()
            forward_copy(m, 0).start()

        for k in range(1, 8):
            sends.append(((group == 1) & has_block, block_copy(m, k)))
        sends.append(((group == 1) & has_block, forward_copy(m, 0)))

    def forward(m):
        @pl.when(group == 1)
        def _():
            for k in (1, 7, 4, 5, 3, 2, 6):
                there = lax.rem(source + k, 8)

                @pl.when(there < BLOCKS)
                def _():
                    arrival(m, BLOCKS * core + there).wait_recv()
                    forward_copy(m, k).start()

            for b in range(BLOCKS):
                arrival(m, BLOCKS * (1 - core) + b).wait_recv()

        for k in range(1, 8):
            sends.append(((group == 1) & (lax.rem(source + k, 8) < BLOCKS), forward_copy(m, k)))

    finisher = owner & (group == 1)

    def finish(m):
        @pl.when(finisher)
        def _():
            r = iota((16 * sections, 1), 0)
            i = r & 7
            token = jnp.where((((r >> 3) & 1) == m) & (i < OWN_TOKENS), OWN_TOKENS * (r >> 4) + i, -5).astype(F32)

            def matches(k):
                ids, live = routed(m, k)
                return token == as_row(padded_column(jnp.where(live, ids, -1.0), -1.0))

            def any_of(hit):
                return jnp.sum(jnp.where(hit, 1.0, 0.0), axis=1, keepdims=True) > 0.5

            last = matches(1)
            in_last = any_of(last)
            first = matches(0)
            in_first = any_of(first)
            base = token == iota((16 * sections, TOK), 1).astype(F32)
            value = (
                dot(onehot(base & ~(in_first | in_last)), tok[m, :, my_columns])
                + dot(onehot(first & ~in_last), blocks[m, my_block])
                + dot(onehot(last), updated[m])
            )
            if m == 0:
                final[...] = value
            else:
                ready[...] = (final[...] + value).astype(BF16).reshape(sections, 16, 128)

    def final_copy(k):
        there = lax.rem(sec + k, sections)
        return remote(ready.at[there], final_in.at[my_block], fin_s.at[k - 1], fin_r.at[my_block], section=there)

    def deliver():
        @pl.when(finisher)
        def _():
            @pl.loop(1, sections)
            def _(k):
                final_copy(k).start()

            final_in[my_block] = ready[sec]

        for b in range(2 * BLOCKS):

            @pl.when(jnp.logical_not(finisher & (my_block == b)))
            def _():
                remote(ready.at[0], final_in.at[b], fin_s.at[0], fin_r.at[b], section=sibling).wait_recv()

            for m in range(MICRO):
                out_ref[m, :, 128 * b : 128 * b + 128] = final_in[b, 8 * m : 8 * m + OWN_TOKENS, :]

    pl.semaphore_wait(barrier, sections + tps - 2)
    broadcast(0)
    forward(0)
    pick(0)
    project(0, 0)
    project(0, 1)
    pass_on(0, 0)
    pass_on(0, 1)
    activate(0, 0)
    broadcast(1)
    forward(1)
    pick(1)
    project(1, 0)
    activate(0, 1)
    project(1, 1)
    pass_on(1, 0)
    pass_on(1, 1)
    down(0)
    activate(1, 0)
    spread(0)
    activate(1, 1)
    combine(0)
    down(1)
    spread(1)
    finish(0)
    combine(1)
    finish(1)
    deliver()

    for condition, copy in sends:
        if condition is None:
            copy.wait_send()
        else:
            pl.when(condition)(copy.wait_send)

    @pl.when(finisher)
    def _():
        @pl.loop(1, sections)
        def _(k):
            final_copy(k).wait_send()


def on_device(*args):
    dma = pltpu.SemaphoreType.DMA
    n = len(CHUNKS)
    return pl.pallas_call(
        body,
        out_shape=jax.ShapeDtypeStruct((MICRO, OWN_TOKENS, Q), BF16),
        in_specs=[pl.BlockSpec(memory_space=pl.ANY)] * 8,
        out_specs=pl.BlockSpec(memory_space=pltpu.VMEM),
        scratch_shapes=[
            pltpu.VMEM((MICRO, TOK, Q), BF16),
            pltpu.VMEM((2, Q), F32),
            pltpu.VMEM((2, Q), F32),
            pltpu.VMEM((Q, HID), BF16),
            pltpu.VMEM((Q, HID), BF16),
            pltpu.VMEM((HID, Q), BF16),
            pltpu.VMEM((MICRO, 2, CAP), jnp.int32),
            pltpu.VMEM((MICRO, 2), jnp.int32),
            pltpu.VMEM((MICRO, ROWS, Q), BF16),
            pltpu.VMEM((MICRO, ROWS, Q), BF16),
            pltpu.VMEM((MICRO, 8, ROWS), F32),
            pltpu.VMEM((MICRO, 3, 8, ROWS), F32),
            pltpu.VMEM((MICRO, 4, 32, 2 * HID), BF16),
            pltpu.VMEM((MICRO, 32, 2 * HID), BF16),
            pltpu.VMEM((MICRO, 2, 32, 2 * HID), BF16),
            pltpu.VMEM((MICRO, 32, 2 * HID), BF16),
            pltpu.VMEM((MICRO, 4, 32, HID), BF16),
            pltpu.VMEM((MICRO, ROWS, HALF), BF16),
            pltpu.VMEM((MICRO, ROWS, HALF), BF16),
            pltpu.VMEM((MICRO, ROWS, HALF), F32),
            pltpu.VMEM((MICRO, 8, ROWS, 128), BF16),
            pltpu.VMEM((MICRO, 7, ROWS, 128), BF16),
            pltpu.VMEM((MICRO, ROWS, 128), BF16),
            pltpu.VMEM((MICRO, 2 * BLOCKS + 1, ROWS, 128), BF16),
            pltpu.VMEM((512, 128), F32),
            pltpu.VMEM((32, 16, 128), BF16),
            pltpu.VMEM((2 * BLOCKS + 1, 16, 128), BF16),
            dma((6 + 2 * n + 1,)),
            dma((MICRO, 3)), dma((MICRO, 3)),
            dma((MICRO, n)), dma((MICRO, n)),
            dma((MICRO, n)), dma((MICRO, n)),
            dma((MICRO, n)), dma((MICRO, n)),
            dma((MICRO, n, 3)), dma((MICRO, n, 3)),
            dma((MICRO,)), dma((MICRO,)),
            dma((MICRO, 7)), dma((MICRO, 7)),
            dma((MICRO,)),
            dma((MICRO, 7)),
            dma((MICRO, 8)),
            dma((MICRO, 2 * BLOCKS + 1)),
            dma((31,)),
            dma((2 * BLOCKS + 1,)),
        ],
        compiler_params=pltpu.CompilerParams(
            collective_id=0, has_side_effects=True, vmem_limit_bytes=60 * 1024 * 1024
        ),
        name="layers",
    )(*args)


def solution(mesh):
    return jax.shard_map(
        on_device,
        mesh=mesh,
        in_specs=(
            P(None, None, "tp"),
            P(None, "tp"),
            P(None, "tp"),
            P("section", "tp", None),
            P("section", "tp", None),
            P("section", None, "tp"),
            P(),
            P(),
        ),
        out_specs=P(None, "section", "tp"),
        check_vma=False,
    )
```

time: 401 us -> 92.8 us (0.23)
  waiting for transfers between devices: 170 us -> 0 us
  Pallas kernels: 0 us -> 91.2 us
  blocking collectives: 78.4 us -> 0 us
  starting transfers between devices: 68.5 us -> 0 us
  other arithmetic: 27.4 us -> 0 us
  matrix products: 20.9 us -> 0 us
  local copies, waits for them, and re-layouts: 21.4 us -> 1.48 us
  between operations: 13.1 us -> 0.01 us
    ppermute x27 -> x0, waiting for transfers between devices: 115 us -> none  [the longest x24 73.8 us: swapped(): return lax.ppermute(value, axis, pairs)]
    pallas_call x0 -> x1, Pallas kernels: none -> 91.2 us  [on_device(): pl.pallas_call(body, out_shape=jax.ShapeDtypeStruct((MICRO, OWN_TOKENS, Q...]
    all_to_all x7 -> x0, blocking collectives: 78.4 us -> none  [the longest x6 46.2 us: from_everyone(): return lax.all_to_all(copies, axis, split_axis=0, concat_axis=0, tiled=True)]
    ppermute x27 -> x0, starting transfers between devices: 68.5 us -> none  [the longest x24 53.5 us: swapped(): return lax.ppermute(value, axis, pairs)]
    while x6 -> x0, waiting for transfers between devices: 55.1 us -> none
    dot_general x9 -> x0, matrix products: 20.9 us -> none  [the longest x3 9.46 us: apply_layer(): gate_part = jnp.dot(scaled, gate_block, preferred_element_type=jnp.float32)]
    while x33 -> x0, local copies, waits for them, and re-layouts: 9.16 us -> none
    select_n x18 -> x0, other arithmetic: 7.93 us -> none  [the longest x3 3.67 us: advance(): current = jnp.where(layer_index == 0, entering, incoming)]
  transfers between devices with their start and end apart: 30 -> 0, of which waited for: 30 -> 0; matrix products, arithmetic and copies ran while one was open for 2% -> 0% of each run, Pallas kernels for 0% -> 0%
where the time goes in v1:
time: 92.8 us; the launch traced here: 92.6 us
  Pallas kernels  91.2 us (98%)
  local copies, waits for them, and re-layouts  1.48 us (2%)
    pallas_call x1, Pallas kernels, on_device(): pl.pallas_call(body, out_shape=jax.ShapeDtypeStruct((MICRO, OWN_TOKENS, Q...  91.2 us

profile of v1, /device:TPU:1, one launch (start us, length us, event | category | flops | bytes accessed | tf_op | source)
XLA Modules:
  0.0 92.6 jit_solution(3700939123531949273)
XLA Ops:
  0.0 91.2 %layers.1 = bf16[2,7,1792]{2,1,0:T(8,128)(2,1)} custom-call(bf16[2,224,1792]{2,1,0:T(8,128)(2,1)} %tok_h.1, f32[2,1792]{1,0:T(2,128)} %gain_h.1, f32[2,1792]{1,0:T(2,128)} %router_h.1, bf16[1,1792,1152]{2,1,0:T(8,128)(2,1)} %wg_h.1, bf16[1,1792,1152]{2,1,0:T(8,128)(2,1)} %wu_h.1, bf16[1,1152,1792]{2,1,0:T(8,128)(2,1)} %wd_h.1, s32[2,2,112]{2,1,0:T(2,128)} %rows_h.1, ...), custom_call_target="tpu_custom_call" | custom-call | tf_op jit(solution)/shard_map/layers/pallas_call | solution.py:459
  91.2 1.5 %copy.9 = bf16[2,7,1792]{2,0,1:T(2,128)(2,1)} copy(bf16[2,7,1792]{2,1,0:T(8,128)(2,1)} %layers.1) | data formatting | bytes 100352 | tf_op jit(solution)/shard_map/layers/pallas_call | solution.py:459

commit v2 on v0

v2 whole, which is shorter than its diff:
```python
import functools

import jax
import jax.numpy as jnp
from jax import lax
from jax.experimental import pallas as pl
from jax.experimental.pallas import tpu as pltpu
from jax.sharding import PartitionSpec as P

MESH = pl.DeviceIdType.MESH
F32 = jnp.float32
BF16 = jnp.bfloat16

MICRO = 2
CAP = 112
TOK = 224
Q = 1792
HID = 1152
D = 7168
EPSILON = 1e-06
GROUP = 32
HALF = Q // 2
BLOCKS = HALF // 128
OWN_TOKENS = 7
CHUNKS = ((0, 512), (512, 640))


def iota(shape, dim):
    return lax.broadcasted_iota(jnp.int32, shape, dim)


def onehot(hit):
    return jnp.where(hit, 1.0, 0.0).astype(BF16)


def as_row(column):
    n = column.shape[0]
    eye = iota((n, n), 0) == iota((n, n), 1)
    return jnp.sum(jnp.where(eye, column, 0.0), axis=0, keepdims=True)


def as_column(row, first=0, n=CAP):
    hit = iota((n, CAP), 1) == iota((n, CAP), 0) + first
    return jnp.sum(jnp.where(hit, row, 0.0), axis=1, keepdims=True)


def dot(a, b):
    return jnp.dot(a, b, preferred_element_type=F32)


def body(
    tok_h, gain_h, router_h, wg_h, wu_h, wd_h, rows_h, cnt_h,
    out_ref,
    tok, gain, router, wg, wu, wd, rows, cnt,
    picked, scaled, stat, stat_in, part, relay, ring, back, hidden, other, xcore, xcore_in, keep,
    summed, summed_in, updated, blocks, news, final, lasts, ready, final_in,
    load_sem, stat_s, stat_r, relay_s, relay_r, ring_s, ring_r, back_s, back_r, hid_s, hid_r,
    core_s, core_r, sum_s, sum_r, hop_s, blk_s, fwd_s, blk_r, fin_s, fin_r,
):
    sec = lax.axis_index("section")
    tp = lax.axis_index("tp")
    core = lax.rem(sec, 2)
    group = sec // 16
    chip = lax.rem(sec, 16) // 2
    ahead = lax.rem(tp + 1 + 2 * core, 4)
    behind = lax.rem(tp + 3 + 2 * core, 4)
    across = lax.rem(tp + 2, 4)
    sibling = sec + 1 - 2 * core
    sections, tps = 32, 4

    barrier = pltpu.get_barrier_semaphore()

    @pl.loop(1, sections)
    def _(k):
        pl.semaphore_signal(
            barrier, inc=1, device_id={"section": lax.rem(sec + k, sections), "tp": tp}, device_id_type=MESH
        )

    for k in range(1, tps):
        pl.semaphore_signal(
            barrier, inc=1, device_id={"section": sec, "tp": lax.rem(tp + k, tps)}, device_id_type=MESH
        )

    loads = []

    def load(src, dst):
        copy = pltpu.make_async_copy(src, dst, load_sem.at[len(loads)])
        copy.start()
        loads.append(copy)
        return copy

    small = [load(rows_h, rows), load(cnt_h, cnt), load(gain_h, gain), load(router_h, router)]
    tok_load = [load(tok_h.at[0], tok.at[0])]
    wgu_load = []
    for start, n in CHUNKS:
        cols = pl.ds(start, n)
        wgu_load.append(
            (load(wg_h.at[0, :, cols], wg.at[:, cols]), load(wu_h.at[0, :, cols], wu.at[:, cols]))
        )
    tok_load.append(load(tok_h.at[1], tok.at[1]))
    wd_load = load(wd_h.at[0], wd)

    @pl.loop(0, MICRO)
    def _(m):
        part[m, tps - 1, CAP - GROUP * (tps - 1) :, :] = jnp.zeros((GROUP * tps - CAP, 2 * HID), BF16)

    def remote(src, dst, ss, rs, section=None, z=None):
        return pltpu.make_async_remote_copy(
            src_ref=src,
            dst_ref=dst,
            send_sem=ss,
            recv_sem=rs,
            device_id={"section": sec if section is None else section, "tp": tp if z is None else z},
            device_id_type=MESH,
        )

    def routed(m, k):
        ids = rows[m, k : k + 1, :].astype(F32)
        count = cnt[m : m + 1, k : k + 1]
        return ids, iota((1, CAP), 1) < count

    owner = chip < BLOCKS
    my_block = BLOCKS * core + chip
    my_columns = pl.ds(pl.multiple_of(128 * jnp.minimum(my_block, 2 * BLOCKS - 1), 128), 128)

    def run(layer):
        sends = []

        def send(copy):
            copy.start()
            sends.append((None, copy))

        def base(m):
            if m == 0:
                for copy in small:
                    copy.wait()
            tok_load[m].wait()
            ids, live = routed(m, layer)
            column = as_column(ids)
            old = column == iota((CAP, TOK), 1).astype(F32)
            if layer == 1:
                ids0, live0 = routed(m, 0)
                new = column == jnp.where(live0, ids0, -2.0)
                old = old & (jnp.sum(jnp.where(new, 1.0, 0.0), axis=1, keepdims=True) < 0.5)
                news[m] = onehot(new)
            old = onehot(old)
            for b in range(Q // 256):
                cols = pl.ds(256 * b, 256)
                picked[m, :, cols] = dot(old, tok[m, :, cols]).astype(BF16)

        def pick(m):
            squares = jnp.zeros((CAP, 256), F32)
            logits = jnp.zeros((CAP, 256), F32)
            for b in range(Q // 256):
                cols = pl.ds(256 * b, 256)
                values = picked[m, :, cols].astype(F32)
                if layer == 1:
                    both = jnp.concatenate([blocks[m, 2 * b], blocks[m, 2 * b + 1]], axis=1)
                    values = values + dot(news[m], both)
                    picked[m, :, cols] = values.astype(BF16)
                squares = squares + values * values
                logits = logits + values * router[layer : layer + 1, cols]
                scaled[m, :, cols] = (values * gain[layer : layer + 1, cols]).astype(BF16)
            squares = as_row(jnp.sum(squares, axis=1, keepdims=True))
            logits = as_row(jnp.sum(logits, axis=1, keepdims=True))
            which = iota((8, CAP), 0)
            stat[m] = jnp.where(which == 0, squares, jnp.where(which == 1, logits, 0.0))

        def stat_copy(m, k):
            return remote(stat.at[m], stat_in.at[m, k - 1], stat_s.at[m, k - 1], stat_r.at[m, k - 1], z=lax.rem(tp + k, tps))

        def send_stats(m):
            for k in range(1, tps):
                send(stat_copy(m, k))

        def spans(n):
            start, width = CHUNKS[n]
            return pl.ds(2 * start, 2 * width), 2 * start, width

        def relay_copy(m, n):
            cols = spans(n)[0]
            return remote(part.at[m, across, :, cols], relay.at[m, :, cols], relay_s.at[m, n], relay_r.at[m, n], z=ahead)

        def back_copy(m, n):
            cols = spans(n)[0]
            return remote(part.at[m, behind, :, cols], back.at[m, :, cols], back_s.at[m, n], back_r.at[m, n], z=behind)

        def ring_copy(m, n):
            cols = spans(n)[0]
            return remote(ring.at[m, 0, :, cols], ring.at[m, 1, :, cols], ring_s.at[m, n], ring_r.at[m, n], z=ahead)

        def store_part(m, first, width, value):
            full = GROUP * (tps - 1)
            part[m, : tps - 1, :, first : first + width] = value[:full].reshape(tps - 1, GROUP, width)
            part[m, tps - 1, : CAP - full, first : first + width] = value[full:]

        def project(m, n):
            start, width = CHUNKS[n]
            if m == 0:
                wgu_load[n][0].wait()
            x = scaled[m]
            gate = dot(x, wg[:, start : start + width]).astype(BF16)
            store_part(m, 2 * start, width, gate)
            if m == 0:
                wgu_load[n][1].wait()
            up = dot(x, wu[:, start : start + width]).astype(BF16)
            store_part(m, 2 * start + width, width, up)

        def launch(m, n):
            if n == 0:
                send_stats(m)
            send(relay_copy(m, n))
            send(back_copy(m, n))

        def pass_on(m, n):
            cols = spans(n)[0]
            relay_copy(m, n).wait_recv()
            ring[m, 0, :, cols] = (part[m, ahead, :, cols].astype(F32) + relay[m, :, cols].astype(F32)).astype(BF16)
            send(ring_copy(m, n))

        def total_stats(m):
            return stat[m] + stat_in[m, 0] + stat_in[m, 1] + stat_in[m, 2]

        def hidden_copy(m, n, k):
            start, width = CHUNKS[n]
            mine = hidden.at[m, tp, :, pl.ds(start, width)]
            return remote(mine, mine, hid_s.at[m, n, k - 1], hid_r.at[m, n, k - 1], z=lax.rem(tp + k, tps))

        def activate(m, n):
            cols, first, width = spans(n)
            start = CHUNKS[n][0]
            if n == 0:
                for k in range(1, tps):
                    stat_copy(m, k).wait_recv()
            back_copy(m, n).wait_recv()
            ring_copy(m, n).wait_recv()
            inverse = lax.rsqrt(as_column(total_stats(m)[0:1], GROUP * tp, GROUP) / D + EPSILON)

            def values(at):
                c = pl.ds(at, width)
                return part[m, tp, :, c].astype(F32) + back[m, :, c].astype(F32) + ring[m, 1, :, c].astype(F32)

            gate = values(first) * inverse
            up = values(first + width) * inverse
            hidden[m, tp, :, start : start + width] = (gate / (1.0 + jnp.exp(-gate)) * up).astype(BF16)
            for k in (2, 1, 3):
                send(hidden_copy(m, n, k))

        def core_copy(m):
            return remote(xcore.at[m], xcore_in.at[m], core_s.at[m], core_r.at[m], section=sibling)

        def down(m, n):
            for k in range(1, tps):
                hidden_copy(m, n, k).wait_recv()
            if m == 0 and n == 0:
                wd_load.wait()
            start, width = CHUNKS[n]
            units = slice(start, start + width)
            x = hidden[m, :, :, units].reshape(GROUP * tps, width)[:CAP]
            theirs = dot(x, wd[units, pl.ds(pl.multiple_of(HALF * (1 - core), 128), HALF)])
            if n == 0:
                other[m] = theirs
            else:
                xcore[m] = (other[m] + theirs).astype(BF16)
                send(core_copy(m))
            mine = dot(x, wd[units, pl.ds(pl.multiple_of(HALF * core, 128), HALF)])
            if n == 0:
                keep[m] = mine
            else:
                keep[m] += mine

        def sum_copy(m, k):
            there = lax.rem(chip + k, 8)
            return there < BLOCKS, remote(
                summed.at[m, there], summed_in.at[m, k - 1], sum_s.at[m, k - 1], sum_r.at[m, k - 1],
                section=16 * group + 2 * there + core,
            )

        def send_if(condition, copy):
            @pl.when(condition)
            def _():
                copy.start()

            sends.append((condition, copy))

        def spread(m):
            core_copy(m).wait_recv()
            for b in range(BLOCKS):
                cols = pl.ds(128 * b, 128)
                summed[m, b] = (keep[m, :, cols] + xcore_in[m, :, cols].astype(F32)).astype(BF16)
            for k in range(1, 8):
                there = lax.rem(chip + k, 8)

                @pl.when(there < BLOCKS)
                def _():
                    sum_copy(m, k)[1].start()

                sends.append((there < BLOCKS, sum_copy(m, k)[1]))


        def hop_copy(m):
            return remote(
                updated.at[m], blocks.at[m, my_block], hop_s.at[m], blk_r.at[m, my_block],
                section=16 + 2 * lax.rem(chip + 4, 8) + core,
            )

        def combine(m):
            @pl.when(owner)
            def _():
                total = summed[m, chip].astype(F32)
                for k in range(1, 8):
                    sum_copy(m, k)[1].wait_recv()
                    total = total + summed_in[m, k - 1].astype(F32)
                logits = as_column(total_stats(m)[1:2])
                gate = 1.0 / (1.0 + jnp.exp(-logits))
                updated[m] = (picked[m, :, my_columns].astype(F32) + gate * total).astype(BF16)

                if layer == 0:
                    hop_copy(m).start()

            if layer == 0:
                sends.append((owner, hop_copy(m)))

        source = lax.rem(chip + 4, 8)
        has_block = source < BLOCKS

        def block_copy(m, k):
            block = BLOCKS * core + source
            return remote(
                blocks.at[m, block], blocks.at[m, block], blk_s.at[m, k - 1], blk_r.at[m, block],
                section=16 + 2 * lax.rem(chip + k, 8) + core,
            )

        def forward_copy(m, k):
            block = BLOCKS * core + lax.rem(source + k, 8)
            return remote(
                blocks.at[m, block], blocks.at[m, block], fwd_s.at[m, k], blk_r.at[m, block], section=sibling
            )

        def arrival(m, block):
            return remote(blocks.at[m, block], blocks.at[m, block], fwd_s.at[m, 0], blk_r.at[m, block], section=sibling)

        def broadcast(m):
            @pl.when(has_block)
            def _():
                arrival(m, BLOCKS * core + source).wait_recv()
                for k in range(1, 8):
                    block_copy(m, k).start()
                forward_copy(m, 0).start()

            for k in range(1, 8):
                sends.append((has_block, block_copy(m, k)))
            sends.append((has_block, forward_copy(m, 0)))

        def forward(m):
            for k in (1, 7, 4, 5, 3, 2, 6):
                there = lax.rem(source + k, 8)

                @pl.when(there < BLOCKS)
                def _():
                    arrival(m, BLOCKS * core + there).wait_recv()
                    forward_copy(m, k).start()

            for b in range(BLOCKS):
                arrival(m, BLOCKS * (1 - core) + b).wait_recv()

            for k in range(1, 8):
                sends.append((lax.rem(source + k, 8) < BLOCKS, forward_copy(m, k)))

        def finish(m):
            @pl.when(owner)
            def _():
                r = iota((16 * sections, 1), 0)
                i = r & 7
                token = jnp.where((((r >> 3) & 1) == m) & (i < OWN_TOKENS), OWN_TOKENS * (r >> 4) + i, -5).astype(F32)

                def matches(k):
                    ids, live = routed(m, k)
                    return token == jnp.where(live, ids, -1.0)

                def any_of(hit):
                    return jnp.sum(jnp.where(hit, 1.0, 0.0), axis=1, keepdims=True) > 0.5

                last = matches(1)
                in_last = any_of(last)
                first = matches(0)
                in_first = any_of(first)
                base = token == iota((16 * sections, TOK), 1).astype(F32)
                value = dot(onehot(base & ~(in_first | in_last)), tok[m, :, my_columns])
                value = value + dot(onehot(first & ~in_last), blocks[m, my_block])
                if m == 0:
                    final[...] = value + dot(onehot(last), updated[m])
                else:
                    final[...] += value
                    lasts[...] = onehot(last)

        def final_copy(k, dy, dx, dc):
            row, column = lax.rem(sec // 8 + dy, 4), lax.rem(chip + dx, 4)
            there = 8 * row + 2 * column + (core if dc == 0 else 1 - core)
            return remote(ready.at[there], final_in.at[my_block], fin_s.at[k], fin_r.at[my_block], section=there)

        def final_copies():
            steps = [(dy, dx, dc) for dy in range(4) for dx in range(4) for dc in range(2)]
            steps.sort(key=lambda o: -(min(o[0], 4 - o[0]) + min(o[1], 4 - o[1])))
            steps.remove((0, 0, 0))
            return [final_copy(k, *step) for k, step in enumerate(steps)]

        def arrived(b):
            remote(ready.at[0], final_in.at[b], fin_s.at[0], fin_r.at[b], section=sibling).wait_recv()

        def deliver():
            if layer == 1:

                @pl.when(owner)
                def _():
                    value = final[...] + dot(lasts[...], updated[MICRO - 1])
                    ready[...] = value.astype(BF16).reshape(sections, 16, 128)

                    for copy in final_copies():
                        copy.start()

                    final_in[my_block] = ready[sec]

            for b in range(2 * BLOCKS):
                if layer == 1:
                    pl.when(jnp.logical_not(owner & (my_block == b)))(functools.partial(arrived, b))
                else:
                    arrived(b)
                for m in range(MICRO):
                    out_ref[:, m, 128 * b : 128 * b + 128] = final_in[b, 8 * m : 8 * m + OWN_TOKENS, :]

        def enter():
            pl.semaphore_wait(barrier, sections + tps - 2)

        orders = (
            (
                (base, 0), (pick, 0), (project, 0, 0), (enter,), (launch, 0, 0), (project, 0, 1), (launch, 0, 1),
                (base, 1), (pick, 1), (project, 1, 0), (project, 1, 1), (pass_on, 0, 0), (pass_on, 0, 1),
                (launch, 1, 0), (activate, 0, 0), (launch, 1, 1), (activate, 0, 1), (pass_on, 1, 0), (pass_on, 1, 1),
                (down, 0, 0), (activate, 1, 0), (down, 0, 1), (spread, 0), (activate, 1, 1), (down, 1, 0),
                (combine, 0), (down, 1, 1), (spread, 1), (combine, 1), (deliver,),
            ),
            (
                (enter,), (base, 0), (base, 1), (broadcast, 0), (forward, 0), (pick, 0), (project, 0, 0),
                (launch, 0, 0), (project, 0, 1), (launch, 0, 1), (broadcast, 1), (pass_on, 0, 0), (pass_on, 0, 1),
                (activate, 0, 0), (forward, 1), (pick, 1), (activate, 0, 1), (project, 1, 0), (launch, 1, 0),
                (project, 1, 1), (launch, 1, 1), (down, 0, 0), (pass_on, 1, 0), (down, 0, 1), (pass_on, 1, 1),
                (spread, 0), (activate, 1, 0), (activate, 1, 1), (down, 1, 0), (combine, 0), (down, 1, 1),
                (spread, 1), (finish, 0), (finish, 1), (combine, 1), (deliver,),
            ),
        )
        for task, *which in orders[layer]:
            with jax.named_scope("_".join([task.__name__, *map(str, which)])):
                task(*which)

        def drain():
            for condition, copy in sends:
                if condition is None:
                    copy.wait_send()
                else:
                    pl.when(condition)(copy.wait_send)

            if layer == 1:

                @pl.when(owner)
                def _():
                    for copy in final_copies():
                        copy.wait_send()

        with jax.named_scope("drain"):
            drain()

    for layer in range(2):
        pl.when(group == layer)(functools.partial(run, layer))


def on_device(*args):
    return jnp.swapaxes(call(*args), 0, 1)


def call(*args):
    dma = pltpu.SemaphoreType.DMA
    n = len(CHUNKS)
    return pl.pallas_call(
        body,
        out_shape=pltpu.VMEM((OWN_TOKENS, MICRO, Q), BF16),
        in_specs=[pl.BlockSpec(memory_space=pl.ANY)] * 8,
        out_specs=pl.BlockSpec(memory_space=pltpu.VMEM),
        scratch_shapes=[
            pltpu.VMEM((MICRO, TOK, Q), BF16),
            pltpu.VMEM((2, Q), F32),
            pltpu.VMEM((2, Q), F32),
            pltpu.VMEM((Q, HID), BF16),
            pltpu.VMEM((Q, HID), BF16),
            pltpu.VMEM((HID, Q), BF16),
            pltpu.VMEM((MICRO, 2, CAP), jnp.int32),
            pltpu.VMEM((MICRO, 2), jnp.int32),
            pltpu.VMEM((MICRO, CAP, Q), BF16),
            pltpu.VMEM((MICRO, CAP, Q), BF16),
            pltpu.VMEM((MICRO, 8, CAP), F32),
            pltpu.VMEM((MICRO, 3, 8, CAP), F32),
            pltpu.VMEM((MICRO, 4, 32, 2 * HID), BF16),
            pltpu.VMEM((MICRO, 32, 2 * HID), BF16),
            pltpu.VMEM((MICRO, 2, 32, 2 * HID), BF16),
            pltpu.VMEM((MICRO, 32, 2 * HID), BF16),
            pltpu.VMEM((MICRO, 4, 32, HID), BF16),
            pltpu.VMEM((MICRO, CAP, HALF), F32),
            pltpu.VMEM((MICRO, CAP, HALF), BF16),
            pltpu.VMEM((MICRO, CAP, HALF), BF16),
            pltpu.VMEM((MICRO, CAP, HALF), F32),
            pltpu.VMEM((MICRO, 8, CAP, 128), BF16),
            pltpu.VMEM((MICRO, 7, CAP, 128), BF16),
            pltpu.VMEM((MICRO, CAP, 128), BF16),
            pltpu.VMEM((MICRO, 2 * BLOCKS + 1, CAP, 128), BF16),
            pltpu.VMEM((MICRO, CAP, CAP), BF16),
            pltpu.VMEM((512, 128), F32),
            pltpu.VMEM((512, CAP), BF16),
            pltpu.VMEM((32, 16, 128), BF16),
            pltpu.VMEM((2 * BLOCKS + 1, 16, 128), BF16),
            dma((6 + 2 * n + 1,)),
            dma((MICRO, 3)), dma((MICRO, 3)),
            dma((MICRO, n)), dma((MICRO, n)),
            dma((MICRO, n)), dma((MICRO, n)),
            dma((MICRO, n)), dma((MICRO, n)),
            dma((MICRO, n, 3)), dma((MICRO, n, 3)),
            dma((MICRO,)), dma((MICRO,)),
            dma((MICRO, 7)), dma((MICRO, 7)),
            dma((MICRO,)),
            dma((MICRO, 7)),
            dma((MICRO, 8)),
            dma((MICRO, 2 * BLOCKS + 1)),
            dma((31,)),
            dma((2 * BLOCKS + 1,)),
        ],
        compiler_params=pltpu.CompilerParams(
            collective_id=0, has_side_effects=True, vmem_limit_bytes=60 * 1024 * 1024
        ),
        name="layers",
    )(*args)


def solution(mesh):
    return jax.shard_map(
        on_device,
        mesh=mesh,
        in_specs=(
            P(None, None, "tp"),
            P(None, "tp"),
            P(None, "tp"),
            P("section", "tp", None),
            P("section", "tp", None),
            P("section", None, "tp"),
            P(),
            P(),
        ),
        out_specs=P(None, "section", "tp"),
        check_vma=False,
    )
```

time: 401 us -> 80.2 us (0.20)
  waiting for transfers between devices: 170 us -> 0 us
  Pallas kernels: 0 us -> 79.4 us
  blocking collectives: 78.4 us -> 0 us
  starting transfers between devices: 68.5 us -> 0 us
  other arithmetic: 27.4 us -> 0 us
  matrix products: 20.9 us -> 0 us
  local copies, waits for them, and re-layouts: 21.4 us -> 0.62 us
  between operations: 13.1 us -> 0.01 us
    ppermute x27 -> x0, waiting for transfers between devices: 115 us -> none  [the longest x24 73.8 us: swapped(): return lax.ppermute(value, axis, pairs)]
    pallas_call x0 -> x1, Pallas kernels: none -> 79.4 us  [call(): pl.pallas_call(body, out_shape=pltpu.VMEM((OWN_TOKENS, MICRO, Q), BF16),...]
    all_to_all x7 -> x0, blocking collectives: 78.4 us -> none  [the longest x6 46.2 us: from_everyone(): return lax.all_to_all(copies, axis, split_axis=0, concat_axis=0, tiled=True)]
    ppermute x27 -> x0, starting transfers between devices: 68.5 us -> none  [the longest x24 53.5 us: swapped(): return lax.ppermute(value, axis, pairs)]
    while x6 -> x0, waiting for transfers between devices: 55.1 us -> none
    dot_general x9 -> x0, matrix products: 20.9 us -> none  [the longest x3 9.46 us: apply_layer(): gate_part = jnp.dot(scaled, gate_block, preferred_element_type=jnp.float32)]
    while x33 -> x0, local copies, waits for them, and re-layouts: 9.16 us -> none
    select_n x18 -> x0, other arithmetic: 7.93 us -> none  [the longest x3 3.67 us: advance(): current = jnp.where(layer_index == 0, entering, incoming)]
  transfers between devices with their start and end apart: 30 -> 0, of which waited for: 30 -> 0; matrix products, arithmetic and copies ran while one was open for 2% -> 0% of each run, Pallas kernels for 0% -> 0%
where the time goes in v2:
time: 80.2 us; the launch traced here: 80.1 us
  Pallas kernels  79.4 us (99%)
    pallas_call x1, Pallas kernels, call(): pl.pallas_call(body, out_shape=pltpu.VMEM((OWN_TOKENS, MICRO, Q), BF16),...  79.4 us

profile of v2, /device:TPU:1, one launch (start us, length us, event | category | flops | bytes accessed | tf_op | source)
XLA Modules:
  0.0 80.1 jit_solution(8434707495733000797)
XLA Ops:
  0.0 79.4 %layers.1 = bf16[7,2,1792]{2,1,0:T(2,128)(2,1)S(1)} custom-call(bf16[2,224,1792]{2,1,0:T(8,128)(2,1)} %tok_h.1, f32[2,1792]{1,0:T(2,128)} %gain_h.1, f32[2,1792]{1,0:T(2,128)} %router_h.1, bf16[1,1792,1152]{2,1,0:T(8,128)(2,1)} %wg_h.1, bf16[1,1792,1152]{2,1,0:T(8,128)(2,1)} %wu_h.1, bf16[1,1152,1792]{2,1,0:T(8,128)(2,1)} %wd_h.1, s32[2,2,112]{2,1,0:T(2,128)} %rows_h.1, ...), custom_call_target="tpu_custom_call" | custom-call | tf_op jit(solution)/shard_map/layers/pallas_call | solution.py:484
  79.4 0.6 copy.10
